TPU v7x, 512 devices: a 4x2x32 block of a 4x8x32 slice. The times are simulated.
512 devices in a mesh: groups: 2 (over y), fsdp: 32 (over z), tensor: 8 (over x, core).
Axes of the slice: x: 4, y: 2, z: 32, core: 2. Of those that a mesh axis runs over, the one named last changes fastest.
The devices are a block of a 4x8x32 slice.
Arguments:
- tokens: bfloat16 [16384, 4608], P(('groups', 'fsdp'), 'tensor'), parts along dimension 0, may hold values from -100 to 100
- norm_gain: bfloat16 [4608], P('tensor'), may hold values from 0.25 to 1.75
- w_query: bfloat16 [4608, 4096], P('fsdp', 'tensor'), may hold values from -0.5 to 0.5
- w_key: bfloat16 [4608, 2048], P('fsdp', 'tensor'), may hold values from -0.09375 to 0.09375
- w_value: bfloat16 [4608, 2048], P('fsdp', 'tensor'), may hold values from -0.09375 to 0.09375
- w_out: bfloat16 [4096, 4608], P('tensor', 'fsdp'), may hold values from -0.5 to 0.5
- post_gain: bfloat16 [4608], P('tensor'), may hold values from 0.25 to 1.75
Outputs:
- mixed: float32 [16384, 4608], P(('groups', 'fsdp'), 'tensor'), parts along dimension 0
There are 2 independent parts, one for each index of `groups`. A program takes and returns all parts, laid end to end along the dimension named above; an argument that names none is the same for every part. Nothing has to cross between parts.
All inputs are finite; a program needn't handle non-finite values.
Results may differ from a plain program's by a relative error of at most 0.0053.
Values may be sent and summed in bfloat16 or wider, within the bound.
A program may use at most 128 MiB of HBM per device.

v0:
```python
import jax
import jax.numpy as jnp
from jax import lax
from jax.sharding import PartitionSpec as P

D = 4608
HEAD_DIM = 128


eps_norm = 1e-06
soft_cap = 50.0
attn_scale = 144.0 ** (-0.5)
rope_base = 10000.0


def copy_for_each(array, axis):
    count = lax.axis_size(axis)
    return lax.all_to_all(
        jnp.broadcast_to(array[None], (count, *array.shape)), axis, 0, 0, tiled=True
    )


def of_everyone(array, axis):
    return copy_for_each(array, axis).sum(axis=0)


def joined_along(pieces, dim):
    pieces = jnp.moveaxis(pieces, 0, dim)
    lengths = pieces.shape
    return pieces.reshape(*lengths[:dim], lengths[dim] * lengths[dim + 1], *lengths[dim + 2 :])


def gather_directly(array, axis, dim):
    return joined_along(copy_for_each(array, axis), dim)


def side_by_side(arrays, axis, dim, along):
    ends, at = ([], 0)
    for a in arrays[:-1]:
        at += a.shape[along]
        ends.append(at)
    both = jnp.concatenate(arrays, axis=along)
    return tuple(jnp.split(lax.all_gather(both, axis, axis=dim, tiled=True), ends, axis=along))


def in_blocks(array, dim, count):
    before, after = (array.shape[:dim], array.shape[dim + 1 :])
    return jnp.moveaxis(array.reshape(*before, count, -1, *after), dim, 0)


def summed_on_arrival(array, axis, dim):
    count = lax.axis_size(axis)
    pieces = lax.all_to_all(in_blocks(array, dim, count), axis, 0, 0, tiled=True)
    return jnp.sum(pieces.astype(jnp.float32), axis=0)


def rotate(values, position):
    head_dim = values.shape[-1]
    half = head_dim // 2
    freq = rope_base ** (-(jnp.arange(half, dtype=jnp.float32) * 2.0 / head_dim))
    angle = position.astype(jnp.float32)[:, None] * freq[None, :]
    cosine = jnp.cos(angle)[:, None, :]
    sine = jnp.sin(angle)[:, None, :]
    first = values[..., :half]
    second = values[..., half:]
    return jnp.concatenate(
        [first * cosine - second * sine, second * cosine + first * sine], axis=-1
    )


def attend(query, keys, values, position):
    count, heads, head_dim = query.shape
    kv_count = keys.shape[1]
    grouped = query.reshape(count, kv_count, heads // kv_count, head_dim)
    scores = (
        jnp.einsum("nkgd,mkd->kgnm", grouped, keys, preferred_element_type=jnp.float32) * attn_scale
    )
    capped = soft_cap * jnp.tanh(scores / soft_cap)
    allowed = position[None, :] <= position[:, None]
    weights = jnp.where(allowed, jnp.exp(capped), 0.0)
    probs = (weights / jnp.sum(weights, axis=-1, keepdims=True)).astype(jnp.bfloat16)
    mixed = jnp.einsum("kgnm,mkd->nkgd", probs, values, preferred_element_type=jnp.float32)
    return mixed.reshape(count, heads * head_dim).astype(jnp.bfloat16)


def on_device(tokens, norm_gain, w_query, w_key, w_value, w_out, post_gain):
    rows = tokens.shape[0]
    local = tokens.astype(jnp.float32)
    total = of_everyone(jnp.sum(local * local, axis=1), "tensor")
    normed = (
        local * lax.rsqrt(total / D + eps_norm)[:, None] * norm_gain.astype(jnp.float32)
    ).astype(jnp.bfloat16)
    whole = gather_directly(normed, "tensor", 1)
    pieces = side_by_side((w_query, w_key, w_value), "fsdp", 0, 1)
    query_raw, key_raw, value_raw = tuple(
        (jnp.dot(whole, piece, preferred_element_type=jnp.float32) for piece in pieces)
    )
    position = jnp.arange(rows, dtype=jnp.int32)
    local_heads = w_query.shape[1] // HEAD_DIM
    local_kv = w_key.shape[1] // HEAD_DIM
    query = rotate(query_raw.reshape(rows, local_heads, HEAD_DIM), position).astype(jnp.bfloat16)
    key = rotate(key_raw.reshape(rows, local_kv, HEAD_DIM), position).astype(jnp.bfloat16)
    value = value_raw.astype(jnp.bfloat16).reshape(rows, local_kv, HEAD_DIM)
    attn = attend(query, key, value, position)
    partial_value = jnp.dot(
        attn, lax.all_gather(w_out, "fsdp", axis=1, tiled=True), preferred_element_type=jnp.float32
    )
    proj = summed_on_arrival(partial_value.astype(jnp.bfloat16), "tensor", 1)
    post_total = of_everyone(jnp.sum(proj * proj, axis=1), "tensor")
    branch = proj * lax.rsqrt(post_total / D + eps_norm)[:, None] * post_gain.astype(jnp.float32)
    return tokens.astype(jnp.float32) + branch


def solution(mesh):
    placed = (
        P(("groups", "fsdp"), "tensor"),
        P("tensor"),
        P("fsdp", "tensor"),
        P("fsdp", "tensor"),
        P("fsdp", "tensor"),
        P("tensor", "fsdp"),
        P("tensor"),
    )
    return jax.shard_map(
        on_device,
        mesh=mesh,
        in_specs=placed,
        out_specs=P(("groups", "fsdp"), "tensor"),
        check_vma=False,
    )
```

profile of v0, /device:TPU:33, one launch (start us, length us, event | category | flops | bytes accessed | tf_op | source)
XLA Modules:
  0.0 380.2 jit_solution(6759158152972305025)
XLA Ops:
  6.5 0.0 all-gather.3.cloned.1.call-start
  6.6 1.7 pad_maximum_fusion
  8.3 0.1 all-gather.3.cloned.1.call-update
  8.3 0.1 all-gather.5.cloned.1.call-start
  8.4 0.7 all-gather.5.cloned.1.call-update
  9.2 1.1 fusion.10
  10.2 0.6 broadcast_in_dim.12
  10.8 44.7 %all-to-all-start = ((f32[8,1,256]{2,1,0:T(1,128)}), f32[8,1,256]{2,1,0:T(1,128)S(1)}, u32[]{:S(2)}, u32[]{:S(2)}) async-start(f32[8,1,256]{2,1,0:T(1,128)} %broadcast_in_dim.12), calls=%async_computation | async-start | bytes 16384 | tf_op jit(solution)/shard_map/all_to_all | solution.py:18
  55.5 0.7 convert_element_type.60
  56.2 4.0 %all-to-all-done = f32[8,1,256]{2,1,0:T(1,128)S(1)} async-done(((f32[8,1,256]{2,1,0:T(1,128)}), f32[8,1,256]{2,1,0:T(1,128)S(1)}, u32[]{:S(2)}, u32[]{:S(2)}) %all-to-all-start) | async-done | bytes 8224 | tf_op jit(solution)/shard_map/all_to_all | solution.py:18
  60.2 1.1 fusion.12
  61.3 1.6 broadcast_in_dim.13
  63.0 4.2 %all-to-all-start.1 = ((bf16[8,256,576]{1,2,0:T(8,128)(2,1)}), bf16[8,256,576]{1,2,0:T(8,128)(2,1)S(1)}, u32[]{:S(2)}, u32[]{:S(2)}) async-start(bf16[8,256,576]{1,2,0:T(8,128)(2,1)} %broadcast_in_dim.13), calls=%async_computation.1 | async-start | bytes 4718592 | tf_op jit(solution)/shard_map/all_to_all | solution.py:18
  67.2 0.3 multiply_cosine_fusion
  67.5 102.3 %all-gather.3.cloned.1.call-done = bf16[4608,1024]{1,0:T(8,128)(2,1)} async-done(((bf16[144,1024]{1,0:T(8,128)(2,1)}), bf16[4608,1024]{1,0:T(8,128)(2,1)}) %all-gather.3.cloned.1.call-update) | async-done | bytes 9437200 | tf_op jit(solution)/shard_map/all_gather | solution.py:43
  169.8 4.8 %slice_bitcast_fusion = bf16[512,4608]{0,1:T(8,128)(2,1)} fusion(bf16[4608,1024]{1,0:T(8,128)(2,1)} %all-gather.3.cloned.1.call-done), kind=kLoop, calls=%fused_computation.1 | loop fusion | bytes 9437184 | tf_op jit(solution)/shard_map/dot_general | solution.py:96
  174.6 6.8 %copy.36 = bf16[512,4608]{1,0:T(8,128)(2,1)} copy(bf16[512,4608]{0,1:T(8,128)(2,1)} %slice_bitcast_fusion) | data formatting | bytes 9437184 | tf_op jit(solution)/shard_map/dot_general | solution.py:96
  181.4 0.0 all-to-all-done.1
  181.4 0.0 copy-start.1
  181.4 4.6 %fusion.22 = f32[256,4,128]{0,2,1:T(8,128)S(1)} fusion(bf16[256,4608,1]{0,1,2:T(8,128)(2,1)S(1)} %bitcast.45, bf16[4,128,4608]{2,1,0:T(8,128)(2,1)} %bitcast.44), kind=kOutput, calls=%fused_computation.44 | convolution fusion | flops 1207959552 | bytes 7602176 | tf_op jit(solution)/shard_map/dot_general | solution.py:96
  186.0 0.0 copy-done.1
  186.0 0.1 subtract_convert_fusion
  186.1 0.2 copy.38
  186.2 0.2 copy.39
  186.4 1.8 slice_bitcast_fusion.1
  188.2 2.6 copy.34
  190.8 3.1 fusion.21
  193.9 0.0 copy-start.2
  194.0 0.6 fusion.6
  194.6 1.1 copy-done.2
  195.6 2.8 fusion.7
  198.4 0.3 convolution_convert_fusion.1
  198.7 103.8 %all-gather.5.cloned.1.call-done = bf16[512,4608]{0,1:T(8,128)(2,1)} async-done(((bf16[512,144]{0,1:T(8,128)(2,1)}), bf16[512,4608]{0,1:T(8,128)(2,1)}) %all-gather.5.cloned.1.call-update) | async-done | bytes 4718608 | tf_op jit(solution)/shard_map/all_gather | solution.py:106
  302.5 3.8 convolution_convert_fusion
  306.3 2.5 copy.42
  308.7 53.6 %all_to_all.22 = bf16[8,256,576]{1,2,0:T(8,128)(2,1)S(1)} all-to-all(bf16[8,256,576]{1,2,0:T(8,128)(2,1)} %bitcast.43), channel_id=1, replica_groups=mesh['groups'=2,'fsdp'=32,'tensor'=8] {'tensor'}, dimensions={0} | all-to-all | bytes 4718592 | tf_op jit(solution)/shard_map/all_to_all | solution.py:53
  362.3 0.0 copy-start.3
  362.3 0.0 copy-start
  362.3 0.3 convert_reduce_fusion
  362.6 0.1 multiply_reduce_fusion
  362.7 0.6 broadcast_in_dim.16
  363.3 4.3 %all-to-all-start.3 = ((f32[8,1,256]{2,1,0:T(1,128)}), f32[8,1,256]{2,1,0:T(1,128)S(1)}, u32[]{:S(2)}, u32[]{:S(2)}) async-start(f32[8,1,256]{2,1,0:T(1,128)} %broadcast_in_dim.16), calls=%async_computation.3 | async-start | bytes 16384 | tf_op jit(solution)/shard_map/all_to_all | solution.py:18
  367.6 0.0 copy-done.3
  367.6 4.7 %all-to-all-done.3 = f32[8,1,256]{2,1,0:T(1,128)S(1)} async-done(((f32[8,1,256]{2,1,0:T(1,128)}), f32[8,1,256]{2,1,0:T(1,128)S(1)}, u32[]{:S(2)}, u32[]{:S(2)}) %all-to-all-start.3) | async-done | bytes 8224 | tf_op jit(solution)/shard_map/all_to_all | solution.py:18
  372.4 0.0 copy-done
  372.4 1.0 convert_add_fusion
  (9 shorter events, 0.2 us)
Async XLA Ops:
  6.5 163.2 %all-gather.3.cloned.1.call-start = ((), (), s32[]{:S(2)}) async-start(), calls=%async_computation.4 | async-start | bytes 9732096 | tf_op jit(solution)/shard_map/all_gather | solution.py:43
  8.3 294.2 %all-gather.5.cloned.1.call-start = ((), (), s32[]{:S(2)}) async-start(), calls=%async_computation.5 | async-start | bytes 4866048 | tf_op jit(solution)/shard_map/all_gather | solution.py:106
  10.8 49.4 %all-to-all-start = ((f32[8,1,256]{2,1,0:T(1,128)}), f32[8,1,256]{2,1,0:T(1,128)S(1)}, u32[]{:S(2)}, u32[]{:S(2)}) async-start(f32[8,1,256]{2,1,0:T(1,128)} %broadcast_in_dim.12), calls=%async_computation | async-start | bytes 16384 | tf_op jit(solution)/shard_map/all_to_all | solution.py:18
  63.0 118.4 %all-to-all-start.1 = ((bf16[8,256,576]{1,2,0:T(8,128)(2,1)}), bf16[8,256,576]{1,2,0:T(8,128)(2,1)S(1)}, u32[]{:S(2)}, u32[]{:S(2)}) async-start(bf16[8,256,576]{1,2,0:T(8,128)(2,1)} %broadcast_in_dim.13), calls=%async_computation.1 | async-start | bytes 4718592 | tf_op jit(solution)/shard_map/all_to_all | solution.py:18
  181.4 4.6 %copy-start.1 = (bf16[8,256,576]{1,2,0:T(8,128)(2,1)}, bf16[8,256,576]{1,2,0:T(8,128)(2,1)S(1)}, u32[]{:S(2)}) copy-start(bf16[8,256,576]{1,2,0:T(8,128)(2,1)S(1)} %all-to-all-done.1) | copy-start | bytes 7077892
  193.9 1.7 copy-start.2
  362.3 5.3 %copy-start.3 = (bf16[576]{0:T(1024)(128)(2,1)S(1)}, bf16[576]{0:T(1024)(128)(2,1)}, u32[]{:S(2)}) copy-start(bf16[576]{0:T(1024)(128)(2,1)} %param.13) | copy-start | bytes 3460
  362.3 10.1 %copy-start = (bf16[256,576]{0,1:T(8,128)(2,1)S(1)}, bf16[256,576]{0,1:T(8,128)(2,1)}, u32[]{:S(2)}) copy-start(bf16[256,576]{0,1:T(8,128)(2,1)} %param.7) | copy-start | bytes 884740
  363.3 9.0 %all-to-all-start.3 = ((f32[8,1,256]{2,1,0:T(1,128)}), f32[8,1,256]{2,1,0:T(1,128)S(1)}, u32[]{:S(2)}, u32[]{:S(2)}) async-start(f32[8,1,256]{2,1,0:T(1,128)} %broadcast_in_dim.16), calls=%async_computation.3 | async-start | bytes 16384 | tf_op jit(solution)/shard_map/all_to_all | solution.py:18
Sparse Core Ops, SparseCore 0:
  9.4 160.3 all-gather.2
  171.9 130.5 all-gather.4
where the time goes:
time: 381 us; the launch traced here: 380 us
  waiting for transfers between devices  216 us (57%)
  blocking collectives  53.6 us (14%)
  starting transfers between devices  53.2 us (14%)
  local copies, waits for them, and re-layouts  22.7 us (6%)
  matrix products  15.1 us (4%)
  between operations  13.6 us (4%)
  other arithmetic  6.51 us (2%)
    all_gather x1, waiting for transfers between devices, on_device(): lax.all_gather(w_out, 'fsdp', axis=1, tiled=True)  104 us
    all_gather x1, waiting for transfers between devices, side_by_side(): lax.all_gather(both, axis, axis=dim, tiled=True)  102 us
    all_to_all x1, blocking collectives, summed_on_arrival(): lax.all_to_all(in_blocks(array, dim, count), axis, 0, 0, tiled=True)  53.6 us
    all_to_all x3, starting transfers between devices, copy_for_each(): lax.all_to_all(jnp.broadcast_to(array[None], (count, *array.shape)), axis...  53.1 us
    dot_general x4, local copies, waits for them, and re-layouts, on_device(): jnp.dot(whole, piece, preferred_element_type=jnp.float32)  16 us
    dot_general x3, matrix products, on_device(): jnp.dot(whole, piece, preferred_element_type=jnp.float32)  10.5 us
    all_to_all x3, waiting for transfers between devices, copy_for_each(): lax.all_to_all(jnp.broadcast_to(array[None], (count, *array.shape)), axis...  8.7 us
  transfers between devices with their start and end apart: 5, of which 4 were waited for; matrix products, arithmetic and copies ran while one was open for 9% of the time, Pallas kernels for 0%

commit v1 on v0

v1 whole, which is shorter than its diff:
```python
import functools

import jax
import jax.numpy as jnp
import numpy as np
from jax import lax
from jax.experimental import pallas as pl
from jax.experimental.pallas import tpu as pltpu
from jax.sharding import PartitionSpec as P

HEAD_DIM = 128
EPS = 1e-06
SOFT_CAP = 50.0
ATTN_SCALE = 144.0 ** (-0.5)
ROPE_BASE = 10000.0
MESH = pl.DeviceIdType.MESH
F32 = jnp.float32
BF16 = jnp.bfloat16

PIECES = 3
EARLY = 5
LAG_B, LAG_C, LAG_D = 6, 10, 14


def nt_dot(a, b):
    return lax.dot_general(a, b, (((1,), (1,)), ((), ())), preferred_element_type=F32)


def kernel(
    nz,
    nt,
    tokens_ref,
    gain_ref,
    wq_ref,
    wk_ref,
    wv_ref,
    wo_ref,
    cos_ref,
    sin_ref,
    proj_ref,
    scale_ref,
    tok,
    gain,
    wo_raw,
    cosine,
    sine,
    wqs,
    wos,
    stage,
    nb,
    acc,
    attn,
    pd,
    ybuf,
    sbuf,
    hbuf,
    xbuf,
    fin,
    nat,
    rout,
    tot,
    tot2,
    lsem,
    zqs,
    zqr,
    zws,
    zwr,
    dqs,
    dqr,
    dws,
    dwr,
    tsend,
    trecv,
    usend,
    urecv,
    n1s,
    n1r,
    n2s,
    n2r,
    psend,
    yrecv,
    drecv,
    hsend,
    hrecv,
    xsend,
    xrecv,
):
    g = lax.axis_index("groups")
    z = lax.axis_index("fsdp")
    t = lax.axis_index("tensor")
    y = lax.rem(g, 2)
    g0 = g - y
    x = t // 2
    c = lax.rem(t, 2)
    nx = nt // 2
    per_t = nz // nt
    half = nz // 2
    rows, width = tok.shape
    d_model = width * nt
    chunk = wqs.shape[2]
    piece = chunk // PIECES
    zn = (lax.rem(z + 1, nz), lax.rem(z + nz - 1, nz))
    xp, xm = lax.rem(x + 1, nx), lax.rem(x + nx - 1, nx)
    peer = (g, z, 2 * x + 1 - c)
    q_last = (half, half - 1)
    w_last = (half - 1, half)

    def local(src, dst, i):
        return pltpu.make_async_copy(src, dst, lsem.at[i])

    def remote(src, dst, ss, rs, dev):
        return pltpu.make_async_remote_copy(
            src_ref=src, dst_ref=dst, send_sem=ss, recv_sem=rs, device_id=dev, device_id_type=MESH
        )

    yq = pl.multiple_of(y * 256, 128)
    yk = pl.multiple_of(y * 128, 128)
    loads = [
        local(wq_ref.at[:, pl.ds(yq, 256)], wqs.at[c, z, :, pl.ds(0, 256)], 0),
        local(wk_ref.at[:, pl.ds(yk, 128)], wqs.at[c, z, :, pl.ds(256, 128)], 1),
        local(wv_ref.at[:, pl.ds(yk, 128)], wqs.at[c, z, :, pl.ds(384, 128)], 2),
        local(tokens_ref, tok, 3),
        local(gain_ref, gain, 4),
        local(wo_ref.at[pl.ds(yq, 256)], wo_raw, 5),
        local(cos_ref, cosine, 6),
        local(sin_ref, sine, 7),
    ]
    for load in loads:
        load.start()

    barrier = pltpu.get_barrier_semaphore()
    partners = [(g, zn[0], t), (g, zn[1], t)]
    partners += [(g, z, lax.rem(t + i, nt)) for i in range(1, nt)]
    partners += [(g0 + 1 - y, z, 2 * x), (g0 + 1 - y, z, 2 * x + 1)]
    for dev in partners:
        pl.semaphore_signal(barrier, inc=1, device_id=dev, device_id_type=MESH)
    pl.semaphore_wait(barrier, len(partners))

    def source(d, k):
        return lax.rem(z - k + nz, nz) if d == 0 else lax.rem(z + k, nz)

    def order(d, k, last):
        if isinstance(k, int) and k == 0:
            return 0
        return 2 * k - 1 if d == 0 or (isinstance(k, int) and k == half) else 2 * k

    def ring_copy(buf, ss, rs, d, k, sem_k, p):
        ref = buf.at[c, source(d, k), pl.ds(p * piece, piece)]
        return remote(ref, ref, ss.at[d, sem_k, p], rs.at[d, sem_k, p], (g, zn[d], t))

    def across(buf, ss, rs, s, i):
        ref = buf.at[c, s]
        return remote(ref, ref, ss.at[i], rs.at[i], peer)

    def across_in(buf, ss, rs, s, i):
        ref = buf.at[1 - c, s]
        return remote(ref, ref, ss.at[i], rs.at[i], peer)

    q_ring = (wqs, zqs, zqr, dqs, dqr, q_last)
    w_ring = (wos, zws, zwr, dws, dwr, w_last)

    def ring_start(ring):
        buf, ss, rs, ds, dr, last = ring
        for p in range(PIECES):
            for d in range(2):
                ring_copy(buf, ss, rs, d, 0, 0, p).start()
        across(buf, ds, dr, z, 0).start()

    def ring_step(ring, k):
        buf, ss, rs, ds, dr, last = ring
        dirs = [d for d in range(2) if not isinstance(k, int) or k <= last[d]]
        for p in range(PIECES):
            for d in dirs:
                ring_copy(buf, ss, rs, d, k, k - 1, p).wait_recv()
                if not isinstance(k, int) or k < last[d]:
                    ring_copy(buf, ss, rs, d, k, k, p).start()
        for d in dirs:
            across(buf, ds, dr, source(d, k), order(d, k, last)).start()

    def across_wait(ring, k):
        buf, ss, rs, ds, dr, last = ring
        for d in range(2):
            if not isinstance(k, int) or k <= last[d]:
                across_in(buf, ds, dr, source(d, k), order(d, k, last)).wait_recv()

    for i in (0, 1, 2):
        loads[i].wait()
    ring_start(q_ring)

    def as_row(column):
        return jnp.broadcast_to(column, (rows, 128)).T[0:8]

    def as_column(row):
        return jnp.broadcast_to(row, (128, rows)).T

    def share(buf, ss, rs):
        return [
            remote(buf.at[t], buf.at[t], ss.at[i], rs.at[t], (g, z, lax.rem(t + i, nt)))
            for i in range(1, nt)
        ]

    def share_wait(buf, ss, rs):
        for i in range(1, nt):
            o = lax.rem(t + nt - i, nt)
            remote(buf.at[o], buf.at[o], ss.at[i], rs.at[o], peer).wait_recv()

    def total_scale(buf):
        total = buf[0, 0:1]
        for i in range(1, nt):
            total = total + buf[i, 0:1]
        return as_column(lax.rsqrt(total / d_model + EPS))

    loads[3].wait()
    values = tok[...].astype(F32)
    tot[t] = as_row(jnp.sum(values * values, axis=1, keepdims=True))
    for copy in share(tot, tsend, trecv):
        copy.start()

    loads[4].wait()
    loads[5].wait()
    wos[c, z] = wo_raw[...].astype(F32).T.astype(BF16)

    def first_hop(to_y):
        return remote(stage, nb.at[t], n1s.at[to_y], n1r.at[c], (g0 + to_y, z, 2 * x + y))

    def normalize():
        share_wait(tot, tsend, trecv)
        scale = total_scale(tot)[:, 0:1]
        stage[...] = (tok[...].astype(F32) * scale * gain[...].astype(F32)).astype(BF16)
        first_hop_other = remote(
            stage, nb.at[t], n1s.at[0], n1r.at[c], (g0 + 1 - y, z, 2 * x + y)
        )
        first_hop_other.start()

        @pl.when(c == y)
        def _():
            nb[t] = stage[...]

        @pl.when(c != y)
        def _():
            remote(stage, nb.at[t], n1s.at[1], n1r.at[c], peer).start()

    def round_x(shard, to, i):
        return remote(
            nb.at[shard], nb.at[shard], n2s.at[i], n2r.at[shard], (g, z, 2 * to + c)
        )

    def first_arrivals():
        for i in range(2):
            shard = 2 * x + i

            @pl.when((y != c) | (c != i))
            def _():
                remote(nb.at[shard], nb.at[shard], n1s.at[0], n1r.at[i], peer).wait_recv()

            round_x(shard, xp, 2 * i).start()
            round_x(shard, xm, 2 * i + 1).start()

    def x_wait(shard):
        round_x(shard, xp, 0).wait_recv()

    def relay():
        x_wait(2 * xm)
        round_x(2 * xm, xp, 4).start()
        x_wait(2 * xp + 1)
        round_x(2 * xp + 1, xm, 5).start()

    def last_arrivals():
        opposite = lax.rem(x + 2, nx)
        x_wait(2 * xm + 1)
        x_wait(2 * xp)
        x_wait(2 * opposite)
        x_wait(2 * opposite + 1)

    first_block = z // per_t

    def block(i, init=False):
        o = lax.rem(first_block + i + nt, nt)
        feats = nb[o]
        for u in range(2):
            w = wqs[u, pl.ds(o * per_t, per_t)].reshape(width, wqs.shape[3])
            part = jnp.dot(feats, w, preferred_element_type=F32)
            acc[u] = part if init else acc[u] + part

    def rotary(values):
        return values * cosine[...] + pltpu.roll(values, HEAD_DIM // 2, 1) * sine[...]

    def attend(u):
        key = rotary(acc[u, :, 256:384]).astype(BF16)
        value = acc[u, :, 384:512].astype(BF16)
        spot_q = lax.broadcasted_iota(jnp.int32, (rows, rows), 0)
        spot_k = lax.broadcasted_iota(jnp.int32, (rows, rows), 1)
        for h in range(2):
            query = rotary(acc[u, :, h * 128 : (h + 1) * 128]).astype(BF16)
            scores = nt_dot(query, key) * ATTN_SCALE
            e = jnp.exp(SOFT_CAP * jnp.tanh(scores / SOFT_CAP))
            e = jnp.where(spot_k <= spot_q, e, 0.0)
            probs = (e / jnp.sum(e, axis=1, keepdims=True)).astype(BF16)
            out = jnp.dot(probs, value, preferred_element_type=F32)
            attn[u, :, h * 128 : (h + 1) * 128] = out.astype(BF16)

    def chunk_of(q):
        k = (q + 1) // 2
        s = lax.rem(jnp.where(lax.rem(q, 2) == 1, z - k + nz, z + k), nz)
        o = s // per_t
        return s, o, o // 2, lax.rem(o, 2)

    def to_peer(s, oc):
        return remote(pd.at[0, s], pd.at[1, s], psend.at[s], drecv.at[s], (g, z, 2 * x + oc))

    def to_pair(s, oc):
        return remote(
            pd.at[0, s], ybuf.at[s], psend.at[s], yrecv.at[s], (g0 + 1 - y, z, 2 * x + oc)
        )

    def stage_a(q):
        s, o, ox, oc = chunk_of(q)
        across_in(wos, dws, dwr, s, q).wait_recv()
        part = nt_dot(wos[0, s], attn[0]) + nt_dot(wos[1, s], attn[1])
        pd[0, s] = part.astype(BF16)

        @pl.when((y == c) & (oc != c))
        def _():
            to_peer(s, oc).start()

        @pl.when(y != c)
        def _():
            to_pair(s, oc).start()

    away = jnp.where(y == c, 0, 1)

    def pair_sum(s):
        to_pair(s, c).wait_recv()

        @pl.when(y != c)
        def _():
            to_peer(s, c).wait_recv()

        return pd[away, s].astype(F32) + ybuf[s].astype(F32)

    def to_side(s, i):
        return remote(
            sbuf.at[s, :, pl.ds(128 * i, 128)],
            hbuf.at[s],
            hsend.at[i, s],
            hrecv.at[s],
            (g, z, 2 * (xp, xm)[i] + c),
        )

    def stage_b(q):
        s, o, ox, oc = chunk_of(q)
        dx = lax.rem(x - ox + nx, nx)

        @pl.when((oc == c) & (dx == 2))
        def _():
            sbuf[s] = pair_sum(s).astype(BF16)
            to_side(s, 0).start()
            to_side(s, 1).start()

    def to_owner(s, side, ox):
        return remote(
            sbuf.at[s], xbuf.at[side, s], xsend.at[s], xrecv.at[side, s], (g, z, 2 * ox + c)
        )

    def stage_c(q):
        s, o, ox, oc = chunk_of(q)
        dx = lax.rem(x - ox + nx, nx)

        @pl.when((oc == c) & ((dx == 1) | (dx == 3)))
        def _():
            total = pair_sum(s)
            to_side(s, 0).wait_recv()
            extra = hbuf[s].astype(F32)
            sbuf[s, :, 0:128] = (total[:, 0:128] + jnp.where(dx == 3, extra, 0.0)).astype(BF16)
            sbuf[s, :, 128:256] = (total[:, 128:256] + jnp.where(dx == 1, extra, 0.0)).astype(BF16)
            to_owner(s, dx // 2, ox).start()

    def stage_d(q):
        s, o, ox, oc = chunk_of(q)

        @pl.when(o == t)
        def _():
            total = pair_sum(s)
            for side in range(2):
                to_owner(s, side, x).wait_recv()
                total = total + xbuf[side, s].astype(F32)
            fin[lax.rem(s, per_t)] = total

    stages = ((stage_a, 0), (stage_b, LAG_B), (stage_c, LAG_C), (stage_d, LAG_D))

    def reduce_chunks(low, high):
        for fn, lag in stages:
            lo, hi = low - lag, high - lag
            if isinstance(lo, int):
                lo, hi = max(lo, 0), max(hi, 0)
            else:
                lo, hi = jnp.maximum(lo, 0), jnp.maximum(hi, 0)

            @pl.loop(lo, hi)
            def _(q):
                fn(q)

    w_start = half - EARLY
    block_after = {
        half - 4: [(0, True), (1, False)],
        half - 3: [(-1, False), (2, False)],
        half - 2: [(-2, False)],
    }
    for k in range(1, half + 1):
        ring_step(q_ring, k)
        if k == w_start:
            ring_start(w_ring)
        if k > w_start:
            ring_step(w_ring, k - w_start)
        if k > 1:
            across_wait(q_ring, k - 1)
        if k == 1:
            across_in(wqs, dqs, dqr, z, 0).wait_recv()
            normalize()
        if k == 3:
            first_arrivals()
        if k == 7:
            relay()
        if k == 11:
            last_arrivals()
        for i, init in block_after.get(k, []):
            block(i, init)

    done = EARLY
    block(3)
    block(-3)
    done += 1
    ring_step(w_ring, done)
    across_wait(q_ring, half)
    block(4)
    loads[6].wait()
    loads[7].wait()
    attend(0)
    done += 1
    ring_step(w_ring, done)
    attend(1)
    done += 1
    ring_step(w_ring, done)

    def ready(i):
        if isinstance(i, int):
            return max(min(4 * (i - done), 2 * i - 1), 0)
        return jnp.maximum(jnp.minimum(4 * (i - done), 2 * i - 1), 0)

    @pl.loop(done + 1, half - 1)
    def _(i):
        ring_step(w_ring, i)
        reduce_chunks(ready(i - 1), ready(i))

    for i in (half - 1, half):
        ring_step(w_ring, i)
        reduce_chunks(ready(i - 1), ready(i))
    at = ready(half)

    @pl.loop(at, nz)
    def _(q):
        stage_a(q)

    for fn, lag in stages[1:]:

        @pl.loop(max(at - lag, 0), nz)
        def _(q):
            fn(q)

    whole = fin[...].reshape(width, rows)
    square = jnp.sum(whole * whole, axis=0, keepdims=True)
    tot2[t] = jnp.broadcast_to(square, (8, rows))
    for copy in share(tot2, usend, urecv):
        copy.start()
    nat[...] = whole.T
    out = local(nat, proj_ref, 8)
    out.start()

    for ring in (q_ring, w_ring):
        buf, ss, rs, ds, dr, last = ring
        for d in range(2):

            @pl.loop(0, last[d])
            def _(k):
                for p in range(PIECES):
                    ring_copy(buf, ss, rs, d, k, k, p).wait_send()

        @pl.loop(0, nz)
        def _(i):
            across(buf, ds, dr, z, i).wait_send()

    for copy in share(tot, tsend, trecv):
        copy.wait_send()
    remote(stage, nb.at[t], n1s.at[0], n1r.at[c], (g0 + 1 - y, z, 2 * x + y)).wait_send()

    @pl.when(c != y)
    def _():
        remote(stage, nb.at[t], n1s.at[1], n1r.at[c], peer).wait_send()

    for i in range(6):
        round_x(0, xp, i).wait_send()

    @pl.loop(0, nz)
    def _(q):
        s, o, ox, oc = chunk_of(q)
        dx = lax.rem(x - ox + nx, nx)

        @pl.when((y != c) | (oc != c))
        def _():
            to_peer(s, 1 - c).wait_send()

        @pl.when((oc == c) & (dx == 2))
        def _():
            to_side(s, 0).wait_send()
            to_side(s, 1).wait_send()

        @pl.when((oc == c) & ((dx == 1) | (dx == 3)))
        def _():
            to_owner(s, 0, xp).wait_send()

    share_wait(tot2, usend, urecv)
    rout[...] = total_scale(tot2)
    out2 = local(rout, scale_ref, 9)
    out2.start()
    for copy in share(tot2, usend, urecv):
        copy.wait_send()
    out.wait()
    out2.wait()


def rope_tables(length):
    half = HEAD_DIM // 2
    freq = np.float32(ROPE_BASE) ** (-(np.arange(half, dtype=np.float32) * np.float32(2.0) / np.float32(HEAD_DIM)))
    angle = np.arange(length, dtype=np.float32)[:, None] * freq.astype(np.float32)[None, :]
    cosine, sine = np.cos(angle), np.sin(angle)
    return (
        np.concatenate([cosine, cosine], axis=1).astype(np.float32),
        np.concatenate([-sine, sine], axis=1).astype(np.float32),
    )


def on_device(nz, nt, tokens, norm_gain, w_query, w_key, w_value, w_out, post_gain):
    rows, width = tokens.shape
    depth = w_query.shape[0]
    cosine, sine = rope_tables(rows)
    q_cols = w_query.shape[1] // 2
    qkv = q_cols + w_key.shape[1] // 2 + w_value.shape[1] // 2
    dma = pltpu.SemaphoreType.DMA
    half = nz // 2
    vm = pltpu.VMEM
    hbm = pl.BlockSpec(memory_space=pl.ANY)
    proj, scale = pl.pallas_call(
        functools.partial(kernel, nz, nt),
        out_shape=(
            jax.ShapeDtypeStruct((rows, width), F32),
            jax.ShapeDtypeStruct((rows, 128), F32),
        ),
        in_specs=[hbm] * 8,
        out_specs=(hbm, hbm),
        scratch_shapes=[
            vm((rows, width), BF16),
            vm((1, width), BF16),
            vm((q_cols, depth), BF16),
            vm((rows, HEAD_DIM), F32),
            vm((rows, HEAD_DIM), F32),
            vm((2, nz, depth, qkv), BF16),
            vm((2, nz, depth, q_cols), BF16),
            vm((rows, width), BF16),
            vm((nt, rows, width), BF16),
            vm((2, rows, qkv), F32),
            vm((2, rows, q_cols), BF16),
            vm((2, nz, depth, rows), BF16),
            vm((nz, depth, rows), BF16),
            vm((nz, depth, rows), BF16),
            vm((nz, depth, 128), BF16),
            vm((2, nz, depth, rows), BF16),
            vm((nz // nt, depth, rows), F32),
            vm((rows, width), F32),
            vm((rows, 128), F32),
            vm((nt, 8, rows), F32),
            vm((nt, 8, rows), F32),
            dma((10,)),
            dma((2, half, PIECES)),
            dma((2, half, PIECES)),
            dma((2, half, PIECES)),
            dma((2, half, PIECES)),
            dma((nz,)),
            dma((nz,)),
            dma((nz,)),
            dma((nz,)),
            dma((nt,)),
            dma((nt,)),
            dma((nt,)),
            dma((nt,)),
            dma((2,)),
            dma((2,)),
            dma((6,)),
            dma((nt,)),
            dma((nz,)),
            dma((nz,)),
            dma((nz,)),
            dma((2, nz)),
            dma((nz,)),
            dma((nz,)),
            dma((2, nz)),
        ],
        compiler_params=pltpu.CompilerParams(
            collective_id=0, has_side_effects=True, vmem_limit_bytes=60 * 1024 * 1024
        ),
        name="attention_block",
    )(
        tokens,
        norm_gain.reshape(1, width),
        w_query,
        w_key,
        w_value,
        w_out,
        jnp.asarray(cosine),
        jnp.asarray(sine),
    )
    branch = proj * scale[:, 0:1] * post_gain.astype(F32)
    return tokens.astype(F32) + branch


def solution(mesh):
    nz, nt = mesh.shape["fsdp"], mesh.shape["tensor"]
    placed = (
        P(("groups", "fsdp"), "tensor"),
        P("tensor"),
        P("fsdp", "tensor"),
        P("fsdp", "tensor"),
        P("fsdp", "tensor"),
        P("tensor", "fsdp"),
        P("tensor"),
    )
    return jax.shard_map(
        functools.partial(on_device, nz, nt),
        mesh=mesh,
        in_specs=placed,
        out_specs=P(("groups", "fsdp"), "tensor"),
        check_vma=False,
    )
```

time: 381 us -> 183 us (0.48)
  waiting for transfers between devices: 216 us -> 0 us
  Pallas kernels: 0 us -> 176 us
  blocking collectives: 53.6 us -> 0 us
  starting transfers between devices: 53.2 us -> 0 us
  local copies, waits for them, and re-layouts: 22.7 us -> 6.01 us
  matrix products: 15.1 us -> 0 us
  between operations: 13.6 us -> 0.04 us
  other arithmetic: 6.51 us -> 1.24 us
    all_gather x2 -> x0, waiting for transfers between devices: 206 us -> none  [the longest x1 104 us: on_device(): lax.all_gather(w_out, 'fsdp', axis=1, tiled=True)]
    pallas_call x0 -> x1, Pallas kernels: none -> 176 us  [on_device(): pl.pallas_call(functools.partial(kernel, nz, nt), out_shape=(jax.ShapeDty...]
    all_to_all x1 -> x0, blocking collectives: 53.6 us -> none  [summed_on_arrival(): lax.all_to_all(in_blocks(array, dim, count), axis, 0, 0, tiled=True)]
    all_to_all x3 -> x0, starting transfers between devices: 53.1 us -> none  [copy_for_each(): lax.all_to_all(jnp.broadcast_to(array[None], (count, *array.shape)), axis...]
    dot_general x4 -> x0, local copies, waits for them, and re-layouts: 16 us -> none  [on_device(): jnp.dot(whole, piece, preferred_element_type=jnp.float32)]
    dot_general x6 -> x0, matrix products: 15.1 us -> none  [the longest x3 10.5 us: on_device(): jnp.dot(whole, piece, preferred_element_type=jnp.float32)]
    all_to_all x3 -> x0, waiting for transfers between devices: 8.7 us -> none  [copy_for_each(): lax.all_to_all(jnp.broadcast_to(array[None], (count, *array.shape)), axis...]
  transfers between devices with their start and end apart: 5 -> 0, of which waited for: 4 -> 0; matrix products, arithmetic and copies ran while one was open for 9% -> 0% of each run, Pallas kernels for 0% -> 0%
where the time goes in v1:
time: 183 us
  Pallas kernels  176 us (96%)
  local copies, waits for them, and re-layouts  6.01 us (3%)
    pallas_call x1, Pallas kernels, on_device(): pl.pallas_call(functools.partial(kernel, nz, nt), out_shape=(jax.ShapeDty...  176 us

profile of v1, /device:TPU:33, one launch (start us, length us, event | category | flops | bytes accessed | tf_op | source)
XLA Modules:
  0.0 183.1 jit_solution(14401766348647471253)
XLA Ops:
  0.0 0.0 copy-start.2
  0.0 0.0 copy-start.1
  0.0 1.3 reshape.4.gain_ref
  1.3 0.0 copy-done.2
  1.3 1.8 copy.16.wo_ref
  3.1 0.0 copy-done.1
  3.1 0.9 copy.14.tokens_ref
  4.0 0.0 copy-start
  4.0 175.8 %attention_block.1 = (f32[256,576]{1,0:T(8,128)}, f32[256,128]{1,0:T(8,128)}) custom-call(bf16[256,576]{1,0:T(8,128)(2,1)} %copy.14.tokens_ref, bf16[1,576]{1,0:T(2,128)(2,1)} %reshape.4.gain_ref, bf16[144,512]{1,0:T(8,128)(2,1)} %wq_ref.1, bf16[144,256]{1,0:T(8,128)(2,1)} %wk_ref.1, bf16[144,256]{1,0:T(8,128)(2,1)} %wv_ref.1, ...), custom_call_target="tpu_custom_call" | custom-call | tf_op jit(solution)/shard_map/attention_block/pallas_call | solution.py:552
  179.8 1.0 slice_reduce_fusion
  180.8 0.0 copy-done
  180.8 1.2 multiply_add_fusion
  182.0 1.0 copy.17
  (1 shorter events, 0.0 us)
Async XLA Ops:
  0.0 1.3 copy-start.2
  0.0 3.1 %copy-start.1 = (bf16[256,576]{0,1:T(8,128)(2,1)S(1)}, bf16[256,576]{0,1:T(8,128)(2,1)}, u32[]{:S(2)}) copy-start(bf16[256,576]{0,1:T(8,128)(2,1)} %param.9) | copy-start | bytes 884740
  4.0 176.8 %copy-start = (bf16[256,576]{1,0:T(8,128)(2,1)S(1)}, bf16[256,576]{1,0:T(8,128)(2,1)}, u32[]{:S(2)}) copy-start(bf16[256,576]{1,0:T(8,128)(2,1)} %copy.14.tokens_ref) | copy-start | bytes 884740

commit v2 on v1

--- a/solution.py
+++ b/solution.py
@@ -18,8 +18,8 @@
 BF16 = jnp.bfloat16
 
 PIECES = 3
-EARLY = 5
-LAG_B, LAG_C, LAG_D = 6, 10, 14
+EARLY = 8
+SLOTS = 4
 
 
 def nt_dot(a, b):
@@ -35,13 +35,14 @@
     wk_ref,
     wv_ref,
     wo_ref,
+    post_ref,
     cos_ref,
     sin_ref,
-    proj_ref,
-    scale_ref,
+    out_ref,
     tok,
     gain,
-    wo_raw,
+    post,
+    pgain,
     cosine,
     sine,
     wqs,
@@ -56,8 +57,7 @@
     hbuf,
     xbuf,
     fin,
-    nat,
-    rout,
+    res,
     tot,
     tot2,
     lsem,
@@ -95,7 +95,7 @@
     nx = nt // 2
     per_t = nz // nt
     half = nz // 2
-    rows, width = tok.shape
+    width, rows = tok.shape
     d_model = width * nt
     chunk = wqs.shape[2]
     piece = chunk // PIECES
@@ -121,9 +121,10 @@
         local(wv_ref.at[:, pl.ds(yk, 128)], wqs.at[c, z, :, pl.ds(384, 128)], 2),
         local(tokens_ref, tok, 3),
         local(gain_ref, gain, 4),
-        local(wo_ref.at[pl.ds(yq, 256)], wo_raw, 5),
+        local(wo_ref.at[:, pl.ds(yq, 256)], wos.at[c, z], 5),
         local(cos_ref, cosine, 6),
         local(sin_ref, sine, 7),
+        local(post_ref, post, 8),
     ]
     for load in loads:
         load.start()
@@ -146,25 +147,40 @@
 
     def ring_copy(buf, ss, rs, d, k, sem_k, p):
         ref = buf.at[c, source(d, k), pl.ds(p * piece, piece)]
-        return remote(ref, ref, ss.at[d, sem_k, p], rs.at[d, sem_k, p], (g, zn[d], t))
-
-    def across(buf, ss, rs, s, i):
-        ref = buf.at[c, s]
-        return remote(ref, ref, ss.at[i], rs.at[i], peer)
+        return remote(ref, ref, ss.at[d, 0, p], rs.at[d, sem_k, p], (g, zn[d], t))
 
     def across_in(buf, ss, rs, s, i):
         ref = buf.at[1 - c, s]
-        return remote(ref, ref, ss.at[i], rs.at[i], peer)
+        return remote(ref, ref, ss.at[0, 0], rs.at[i], peer)
 
     q_ring = (wqs, zqs, zqr, dqs, dqr, q_last)
     w_ring = (wos, zws, zwr, dws, dwr, w_last)
 
+    def slot(k):
+        return k % SLOTS if isinstance(k, int) else lax.rem(k, SLOTS)
+
+    def ring_send(ring, d, k, p):
+        buf, ss, rs, ds, dr, last = ring
+        ref = buf.at[c, source(d, k), pl.ds(p * piece, piece)]
+        return remote(ref, ref, ss.at[d, slot(k), p], rs.at[d, k, p], (g, zn[d], t))
+
+    def across_send(ring, d, k):
+        buf, ss, rs, ds, dr, last = ring
+        ref = buf.at[c, source(d, k)]
+        return remote(ref, ref, ds.at[d, slot(k)], dr.at[order(d, k, last)], peer)
+
+    def guarded(k, fn):
+        if isinstance(k, int):
+            if k >= SLOTS:
+                fn()
+        else:
+            pl.when(k >= SLOTS)(fn)
+
     def ring_start(ring):
-        buf, ss, rs, ds, dr, last = ring
         for p in range(PIECES):
             for d in range(2):
-                ring_copy(buf, ss, rs, d, 0, 0, p).start()
-        across(buf, ds, dr, z, 0).start()
+                ring_send(ring, d, 0, p).start()
+        across_send(ring, 0, 0).start()
 
     def ring_step(ring, k):
         buf, ss, rs, ds, dr, last = ring
@@ -173,9 +189,26 @@
             for d in dirs:
                 ring_copy(buf, ss, rs, d, k, k - 1, p).wait_recv()
                 if not isinstance(k, int) or k < last[d]:
-                    ring_copy(buf, ss, rs, d, k, k, p).start()
+                    guarded(k, lambda: ring_send(ring, d, k, p).wait_send())
+                    ring_send(ring, d, k, p).start()
         for d in dirs:
-            across(buf, ds, dr, source(d, k), order(d, k, last)).start()
+            if d == 0:
+                guarded(k, lambda: across_send(ring, d, k).wait_send())
+            elif isinstance(k, int):
+                if k > SLOTS:
+                    across_send(ring, d, k).wait_send()
+            else:
+                pl.when(k > SLOTS)(lambda: across_send(ring, d, k).wait_send())
+            across_send(ring, d, k).start()
+
+    def ring_drain(ring):
+        buf, ss, rs, ds, dr, last = ring
+        for d in range(2):
+            for k in range(last[d] - SLOTS, last[d]):
+                for p in range(PIECES):
+                    ring_send(ring, d, k, p).wait_send()
+            for k in range(last[d] - SLOTS + 1, last[d] + 1):
+                across_send(ring, d, k).wait_send()
 
     def across_wait(ring, k):
         buf, ss, rs, ds, dr, last = ring
@@ -187,12 +220,6 @@
         loads[i].wait()
     ring_start(q_ring)
 
-    def as_row(column):
-        return jnp.broadcast_to(column, (rows, 128)).T[0:8]
-
-    def as_column(row):
-        return jnp.broadcast_to(row, (128, rows)).T
-
     def share(buf, ss, rs):
         return [
             remote(buf.at[t], buf.at[t], ss.at[i], rs.at[t], (g, z, lax.rem(t + i, nt)))
@@ -208,25 +235,26 @@
         total = buf[0, 0:1]
         for i in range(1, nt):
             total = total + buf[i, 0:1]
-        return as_column(lax.rsqrt(total / d_model + EPS))
+        return lax.rsqrt(total / d_model + EPS)
 
     loads[3].wait()
     values = tok[...].astype(F32)
-    tot[t] = as_row(jnp.sum(values * values, axis=1, keepdims=True))
+    tot[t] = jnp.broadcast_to(jnp.sum(values * values, axis=0, keepdims=True), (8, rows))
     for copy in share(tot, tsend, trecv):
         copy.start()
 
     loads[4].wait()
     loads[5].wait()
-    wos[c, z] = wo_raw[...].astype(F32).T.astype(BF16)
+    loads[8].wait()
+    pgain[...] = jnp.broadcast_to(post[...].astype(F32).reshape(1, width), (128, width)).T
 
     def first_hop(to_y):
         return remote(stage, nb.at[t], n1s.at[to_y], n1r.at[c], (g0 + to_y, z, 2 * x + y))
 
     def normalize():
         share_wait(tot, tsend, trecv)
-        scale = total_scale(tot)[:, 0:1]
-        stage[...] = (tok[...].astype(F32) * scale * gain[...].astype(F32)).astype(BF16)
+        scaled = (tok[...].astype(F32) * total_scale(tot)).T
+        stage[...] = (scaled * gain[...].astype(F32).reshape(1, width)).astype(BF16)
         first_hop_other = remote(
             stage, nb.at[t], n1s.at[0], n1r.at[c], (g0 + 1 - y, z, 2 * x + y)
         )
@@ -305,12 +333,21 @@
         o = s // per_t
         return s, o, o // 2, lax.rem(o, 2)
 
+    def owned(s):
+        return s // (2 * per_t) * per_t + lax.rem(s, per_t)
+
     def to_peer(s, oc):
-        return remote(pd.at[0, s], pd.at[1, s], psend.at[s], drecv.at[s], (g, z, 2 * x + oc))
+        return remote(
+            pd.at[0, s], pd.at[1, s], psend.at[s], drecv.at[owned(s)], (g, z, 2 * x + oc)
+        )
 
     def to_pair(s, oc):
         return remote(
-            pd.at[0, s], ybuf.at[s], psend.at[s], yrecv.at[s], (g0 + 1 - y, z, 2 * x + oc)
+            pd.at[0, s],
+            ybuf.at[s],
+            psend.at[s],
+            yrecv.at[owned(s)],
+            (g0 + 1 - y, z, 2 * x + oc),
         )
 
     def stage_a(q):
@@ -342,8 +379,8 @@
         return remote(
             sbuf.at[s, :, pl.ds(128 * i, 128)],
             hbuf.at[s],
-            hsend.at[i, s],
-            hrecv.at[s],
+            hsend.at[i, lax.rem(s, per_t)],
+            hrecv.at[i, lax.rem(s, per_t)],
             (g, z, 2 * (xp, xm)[i] + c),
         )
 
@@ -359,7 +396,11 @@
 
     def to_owner(s, side, ox):
         return remote(
-            sbuf.at[s], xbuf.at[side, s], xsend.at[s], xrecv.at[side, s], (g, z, 2 * ox + c)
+            sbuf.at[s],
+            xbuf.at[side, s],
+            xsend.at[side, lax.rem(s, per_t)],
+            xrecv.at[side, lax.rem(s, per_t)],
+            (g, z, 2 * ox + c),
         )
 
     def stage_c(q):
@@ -369,7 +410,14 @@
         @pl.when((oc == c) & ((dx == 1) | (dx == 3)))
         def _():
             total = pair_sum(s)
-            to_side(s, 0).wait_recv()
+            @pl.when(dx == 3)
+            def _():
+                to_side(s, 0).wait_recv()
+
+            @pl.when(dx == 1)
+            def _():
+                to_side(s, 1).wait_recv()
+
             extra = hbuf[s].astype(F32)
             sbuf[s, :, 0:128] = (total[:, 0:128] + jnp.where(dx == 3, extra, 0.0)).astype(BF16)
             sbuf[s, :, 128:256] = (total[:, 128:256] + jnp.where(dx == 1, extra, 0.0)).astype(BF16)
@@ -386,15 +434,18 @@
                 total = total + xbuf[side, s].astype(F32)
             fin[lax.rem(s, per_t)] = total
 
-    stages = ((stage_a, 0), (stage_b, LAG_B), (stage_c, LAG_C), (stage_d, LAG_D))
+    def clipped(value, low, high):
+        if isinstance(value, int):
+            return max(min(value, high), low)
+        return jnp.maximum(jnp.minimum(value, high), low)
+
+    def reached(i):
+        a = clipped(8 * (i - EARLY), 0, 2 * i - 1)
+        b = clipped(4 * (i - EARLY) - 8, 0, a)
+        return a, b, clipped(b - 4, 0, b), clipped(b - 8, 0, b)
 
     def reduce_chunks(low, high):
-        for fn, lag in stages:
-            lo, hi = low - lag, high - lag
-            if isinstance(lo, int):
-                lo, hi = max(lo, 0), max(hi, 0)
-            else:
-                lo, hi = jnp.maximum(lo, 0), jnp.maximum(hi, 0)
+        for fn, lo, hi in zip((stage_a, stage_b, stage_c, stage_d), low, high):
 
             @pl.loop(lo, hi)
             def _(q):
@@ -417,77 +468,49 @@
         if k == 1:
             across_in(wqs, dqs, dqr, z, 0).wait_recv()
             normalize()
-        if k == 3:
+        if k == 5:
             first_arrivals()
-        if k == 7:
+        if k == 8:
             relay()
         if k == 11:
             last_arrivals()
         for i, init in block_after.get(k, []):
             block(i, init)
 
-    done = EARLY
     block(3)
     block(-3)
-    done += 1
-    ring_step(w_ring, done)
     across_wait(q_ring, half)
     block(4)
     loads[6].wait()
     loads[7].wait()
     attend(0)
-    done += 1
-    ring_step(w_ring, done)
     attend(1)
-    done += 1
-    ring_step(w_ring, done)
-
-    def ready(i):
-        if isinstance(i, int):
-            return max(min(4 * (i - done), 2 * i - 1), 0)
-        return jnp.maximum(jnp.minimum(4 * (i - done), 2 * i - 1), 0)
-
-    @pl.loop(done + 1, half - 1)
+
+    @pl.loop(EARLY + 1, half - 1)
     def _(i):
         ring_step(w_ring, i)
-        reduce_chunks(ready(i - 1), ready(i))
+        reduce_chunks(reached(i - 1), reached(i))
 
     for i in (half - 1, half):
         ring_step(w_ring, i)
-        reduce_chunks(ready(i - 1), ready(i))
-    at = ready(half)
-
-    @pl.loop(at, nz)
+        reduce_chunks(reached(i - 1), reached(i))
+    at = reached(half)
+
+    @pl.loop(at[0], nz)
     def _(q):
         stage_a(q)
 
-    for fn, lag in stages[1:]:
-
-        @pl.loop(max(at - lag, 0), nz)
-        def _(q):
-            fn(q)
+    ring_drain(q_ring)
+    ring_drain(w_ring)
+
+    reduce_chunks((nz,) + at[1:], (nz,) * 4)
 
     whole = fin[...].reshape(width, rows)
     square = jnp.sum(whole * whole, axis=0, keepdims=True)
     tot2[t] = jnp.broadcast_to(square, (8, rows))
     for copy in share(tot2, usend, urecv):
         copy.start()
-    nat[...] = whole.T
-    out = local(nat, proj_ref, 8)
-    out.start()
-
-    for ring in (q_ring, w_ring):
-        buf, ss, rs, ds, dr, last = ring
-        for d in range(2):
-
-            @pl.loop(0, last[d])
-            def _(k):
-                for p in range(PIECES):
-                    ring_copy(buf, ss, rs, d, k, k, p).wait_send()
-
-        @pl.loop(0, nz)
-        def _(i):
-            across(buf, ds, dr, z, i).wait_send()
+    res[...] = whole * pgain[:, 0:1]
 
     for copy in share(tot, tsend, trecv):
         copy.wait_send()
@@ -499,6 +522,11 @@
 
     for i in range(6):
         round_x(0, xp, i).wait_send()
+
+    share_wait(tot2, usend, urecv)
+    res[...] = tok[...].astype(F32) + res[...] * total_scale(tot2)
+    out = local(res, out_ref, 9)
+    out.start()
 
     @pl.loop(0, nz)
     def _(q):
@@ -516,16 +544,11 @@
 
         @pl.when((oc == c) & ((dx == 1) | (dx == 3)))
         def _():
-            to_owner(s, 0, xp).wait_send()
-
-    share_wait(tot2, usend, urecv)
-    rout[...] = total_scale(tot2)
-    out2 = local(rout, scale_ref, 9)
-    out2.start()
+            to_owner(s, dx // 2, xp).wait_send()
+
     for copy in share(tot2, usend, urecv):
         copy.wait_send()
     out.wait()
-    out2.wait()
 
 
 def rope_tables(length):
@@ -549,18 +572,16 @@
     half = nz // 2
     vm = pltpu.VMEM
     hbm = pl.BlockSpec(memory_space=pl.ANY)
-    proj, scale = pl.pallas_call(
+    out = pl.pallas_call(
         functools.partial(kernel, nz, nt),
-        out_shape=(
-            jax.ShapeDtypeStruct((rows, width), F32),
-            jax.ShapeDtypeStruct((rows, 128), F32),
-        ),
-        in_specs=[hbm] * 8,
-        out_specs=(hbm, hbm),
+        out_shape=jax.ShapeDtypeStruct((width, rows), F32),
+        in_specs=[hbm] * 9,
+        out_specs=hbm,
         scratch_shapes=[
-            vm((rows, width), BF16),
-            vm((1, width), BF16),
-            vm((q_cols, depth), BF16),
+            vm((width, rows), BF16),
+            vm((width,), BF16),
+            vm((width,), BF16),
+            vm((width, 128), F32),
             vm((rows, HEAD_DIM), F32),
             vm((rows, HEAD_DIM), F32),
             vm((2, nz, depth, qkv), BF16),
@@ -575,18 +596,17 @@
             vm((nz, depth, 128), BF16),
             vm((2, nz, depth, rows), BF16),
             vm((nz // nt, depth, rows), F32),
-            vm((rows, width), F32),
-            vm((rows, 128), F32),
+            vm((width, rows), F32),
             vm((nt, 8, rows), F32),
             vm((nt, 8, rows), F32),
             dma((10,)),
+            dma((2, SLOTS, PIECES)),
             dma((2, half, PIECES)),
+            dma((2, SLOTS, PIECES)),
             dma((2, half, PIECES)),
-            dma((2, half, PIECES)),
-            dma((2, half, PIECES)),
+            dma((2, SLOTS)),
             dma((nz,)),
-            dma((nz,)),
-            dma((nz,)),
+            dma((2, SLOTS)),
             dma((nz,)),
             dma((nt,)),
             dma((nt,)),
@@ -597,29 +617,29 @@
             dma((6,)),
             dma((nt,)),
             dma((nz,)),
-            dma((nz,)),
-            dma((nz,)),
-            dma((2, nz)),
-            dma((nz,)),
-            dma((nz,)),
-            dma((2, nz)),
+            dma((nz // 2,)),
+            dma((nz // 2,)),
+            dma((2, nz // nt)),
+            dma((2, nz // nt)),
+            dma((2, nz // nt)),
+            dma((2, nz // nt)),
         ],
         compiler_params=pltpu.CompilerParams(
             collective_id=0, has_side_effects=True, vmem_limit_bytes=60 * 1024 * 1024
         ),
         name="attention_block",
     )(
-        tokens,
-        norm_gain.reshape(1, width),
+        tokens.T,
+        norm_gain,
         w_query,
         w_key,
         w_value,
-        w_out,
+        w_out.T,
+        post_gain,
         jnp.asarray(cosine),
         jnp.asarray(sine),
     )
-    branch = proj * scale[:, 0:1] * post_gain.astype(F32)
-    return tokens.astype(F32) + branch
+    return out.T
 
 
 def solution(mesh):

time: 183 us -> 171 us (0.934)
  Pallas kernels: 176 us -> 169 us
  local copies, waits for them, and re-layouts: 6.01 us -> 1.92 us
    pallas_call x1, Pallas kernels: 176 us -> 169 us  [on_device(): pl.pallas_call(functools.partial(kernel, nz, nt), out_shape=jax.ShapeDtyp...]
where the time goes in v2:
time: 171 us
  Pallas kernels  169 us (99%)
  local copies, waits for them, and re-layouts  1.92 us (1%)
    pallas_call x1, Pallas kernels, on_device(): pl.pallas_call(functools.partial(kernel, nz, nt), out_shape=jax.ShapeDtyp...  169 us

profile of v2, /device:TPU:33, one launch (start us, length us, event | category | flops | bytes accessed | tf_op | source)
XLA Modules:
  0.0 171.2 jit_solution(3304217579645473215)
XLA Ops:
  0.0 169.2 %attention_block.1 = f32[576,256]{1,0:T(8,128)} custom-call(bf16[576,256]{1,0:T(8,128)(2,1)} %bitcast.4, bf16[576]{0:T(1024)(128)(2,1)} %gain_ref.1, bf16[144,512]{1,0:T(8,128)(2,1)} %wq_ref.1, bf16[144,256]{1,0:T(8,128)(2,1)} %wk_ref.1, bf16[144,256]{1,0:T(8,128)(2,1)} %wv_ref.1, bf16[144,512]{1,0:T(8,128)(2,1)} %bitcast.5, bf16[576]{0:T(1024)(128)(2,1)} %post_ref.1, ...), custom_call_target="tpu_custom_call" | custom-call | tf_op jit(solution)/shard_map/attention_block/pallas_call | solution.py:575
  169.2 1.9 %copy.11 = f32[256,576]{0,1:T(8,128)} copy(f32[256,576]{0,1:T(8,128)} %bitcast.3) | data formatting | bytes 1179648

commit v3 on v2

--- a/solution.py
+++ b/solution.py
@@ -18,7 +18,7 @@
 BF16 = jnp.bfloat16
 
 PIECES = 3
-EARLY = 8
+EARLY = 11
 SLOTS = 4
 
 
@@ -55,6 +55,7 @@
     ybuf,
     sbuf,
     hbuf,
+    abuf,
     xbuf,
     fin,
     res,
@@ -82,6 +83,7 @@
     drecv,
     hsend,
     hrecv,
+    arecv,
     xsend,
     xrecv,
 ):
@@ -355,12 +357,23 @@
         across_in(wos, dws, dwr, s, q).wait_recv()
         part = nt_dot(wos[0, s], attn[0]) + nt_dot(wos[1, s], attn[1])
         pd[0, s] = part.astype(BF16)
-
-        @pl.when((y == c) & (oc != c))
+        dx = lax.rem(x - ox + nx, nx)
+
+        @pl.when((dx == 2) & (y == c))
+        def _():
+            to_side(s, 0, oc).start()
+            to_side(s, 1, oc).start()
+
+        @pl.when((dx == 2) & (y != c))
+        def _():
+            to_side_away(s, 0).start()
+            to_side_away(s, 1).start()
+
+        @pl.when((dx != 2) & (y == c) & (oc != c))
         def _():
             to_peer(s, oc).start()
 
-        @pl.when(y != c)
+        @pl.when((dx == 0) & (y != c))
         def _():
             to_pair(s, oc).start()
 
@@ -375,24 +388,37 @@
 
         return pd[away, s].astype(F32) + ybuf[s].astype(F32)
 
-    def to_side(s, i):
+    def to_side(s, i, oc):
         return remote(
-            sbuf.at[s, :, pl.ds(128 * i, 128)],
+            pd.at[0, s, :, pl.ds(128 * i, 128)],
             hbuf.at[s],
-            hsend.at[i, lax.rem(s, per_t)],
+            hsend.at[i, lax.rem(s, 2 * per_t)],
             hrecv.at[i, lax.rem(s, per_t)],
+            (g, z, 2 * (xp, xm)[i] + oc),
+        )
+
+    def to_side_away(s, i):
+        return remote(
+            pd.at[0, s, :, pl.ds(128 * i, 128)],
+            abuf.at[s],
+            hsend.at[i, lax.rem(s, 2 * per_t)],
+            arecv.at[i, lax.rem(s, 2 * per_t)],
             (g, z, 2 * (xp, xm)[i] + c),
         )
 
     def stage_b(q):
         s, o, ox, oc = chunk_of(q)
         dx = lax.rem(x - ox + nx, nx)
-
-        @pl.when((oc == c) & (dx == 2))
-        def _():
-            sbuf[s] = pair_sum(s).astype(BF16)
-            to_side(s, 0).start()
-            to_side(s, 1).start()
+        for i in range(2):
+
+            @pl.when((y != c) & (dx == 3 - 2 * i))
+            def _():
+                to_side_away(s, i).wait_recv()
+                span = slice(128 * i, 128 * i + 128)
+                pd[0, s, :, span] = (
+                    pd[0, s, :, span].astype(F32) + abuf[s].astype(F32)
+                ).astype(BF16)
+                to_pair(s, oc).start()
 
     def to_owner(s, side, ox):
         return remote(
@@ -412,11 +438,11 @@
             total = pair_sum(s)
             @pl.when(dx == 3)
             def _():
-                to_side(s, 0).wait_recv()
+                to_side(s, 0, c).wait_recv()
 
             @pl.when(dx == 1)
             def _():
-                to_side(s, 1).wait_recv()
+                to_side(s, 1, c).wait_recv()
 
             extra = hbuf[s].astype(F32)
             sbuf[s, :, 0:128] = (total[:, 0:128] + jnp.where(dx == 3, extra, 0.0)).astype(BF16)
@@ -441,8 +467,9 @@
 
     def reached(i):
         a = clipped(8 * (i - EARLY), 0, 2 * i - 1)
-        b = clipped(4 * (i - EARLY) - 8, 0, a)
-        return a, b, clipped(b - 4, 0, b), clipped(b - 8, 0, b)
+        before = clipped(8 * (i - 1 - EARLY), 0, 2 * i - 3)
+        b = clipped(4 * (i - 1 - EARLY), 0, before)
+        return a, b, clipped(5 * (i - EARLY) - 16, 0, b), clipped(5 * (i - EARLY) - 22, 0, b)
 
     def reduce_chunks(low, high):
         for fn, lo, hi in zip((stage_a, stage_b, stage_c, stage_d), low, high):
@@ -533,14 +560,14 @@
         s, o, ox, oc = chunk_of(q)
         dx = lax.rem(x - ox + nx, nx)
 
-        @pl.when((y != c) | (oc != c))
+        @pl.when((dx != 2) & ((y != c) | (oc != c)))
         def _():
             to_peer(s, 1 - c).wait_send()
 
-        @pl.when((oc == c) & (dx == 2))
-        def _():
-            to_side(s, 0).wait_send()
-            to_side(s, 1).wait_send()
+        @pl.when(dx == 2)
+        def _():
+            to_side(s, 0, c).wait_send()
+            to_side(s, 1, c).wait_send()
 
         @pl.when((oc == c) & ((dx == 1) | (dx == 3)))
         def _():
@@ -594,6 +621,7 @@
             vm((nz, depth, rows), BF16),
             vm((nz, depth, rows), BF16),
             vm((nz, depth, 128), BF16),
+            vm((nz, depth, 128), BF16),
             vm((2, nz, depth, rows), BF16),
             vm((nz // nt, depth, rows), F32),
             vm((width, rows), F32),
@@ -619,8 +647,9 @@
             dma((nz,)),
             dma((nz // 2,)),
             dma((nz // 2,)),
+            dma((2, 2 * nz // nt)),
             dma((2, nz // nt)),
-            dma((2, nz // nt)),
+            dma((2, 2 * nz // nt)),
             dma((2, nz // nt)),
             dma((2, nz // nt)),
         ],

time: 171 us -> 166 us (0.971)
  Pallas kernels: 169 us -> 163 us
    pallas_call x1, Pallas kernels: 169 us -> 163 us  [on_device(): pl.pallas_call(functools.partial(kernel, nz, nt), out_shape=jax.ShapeDtyp...]
where the time goes in v3:
time: 166 us; the launch traced here: 165 us
  Pallas kernels  163 us (98%)
  local copies, waits for them, and re-layouts  1.92 us (1%)
    pallas_call x1, Pallas kernels, on_device(): pl.pallas_call(functools.partial(kernel, nz, nt), out_shape=jax.ShapeDtyp...  163 us

profile of v3, /device:TPU:33, one launch (start us, length us, event | category | flops | bytes accessed | tf_op | source)
XLA Modules:
  0.0 165.4 jit_solution(17960992809018675895)
XLA Ops:
  0.0 163.4 %attention_block.1 = f32[576,256]{1,0:T(8,128)} custom-call(bf16[576,256]{1,0:T(8,128)(2,1)} %bitcast.4, bf16[576]{0:T(1024)(128)(2,1)} %gain_ref.1, bf16[144,512]{1,0:T(8,128)(2,1)} %wq_ref.1, bf16[144,256]{1,0:T(8,128)(2,1)} %wk_ref.1, bf16[144,256]{1,0:T(8,128)(2,1)} %wv_ref.1, bf16[144,512]{1,0:T(8,128)(2,1)} %bitcast.5, bf16[576]{0:T(1024)(128)(2,1)} %post_ref.1, ...), custom_call_target="tpu_custom_call" | custom-call | tf_op jit(solution)/shard_map/attention_block/pallas_call | solution.py:602
  163.4 1.9 %copy.11 = f32[256,576]{0,1:T(8,128)} copy(f32[256,576]{0,1:T(8,128)} %bitcast.3) | data formatting | bytes 1179648
